TPU v7x, 16 devices: a whole 2x2x2 slice. The times are simulated.
16 devices in a mesh: nodes: 16 (over z, y, x, core).
Axes of the slice: x: 2, y: 2, z: 2, core: 2. Of those that a mesh axis runs over, the one named last changes fastest.
Arguments:
- adjacency: bfloat16 [16384, 16384], P('nodes')
- features: bfloat16 [16384, 602], P('nodes')
- w_one: float32 [602, 128], replicated
- w_two: float32 [128, 41], replicated
- labels: int32 [16384], P('nodes')
- label_mask: int32 [16384], P('nodes')
Outputs:
- output 1: float32 [1], replicated
- output 2: float32 [602, 128], replicated
- output 3: float32 [128, 41], replicated
All inputs are finite; a program needn't handle non-finite values.
Results may differ from a plain program's by a relative error of at most 0.001.
Values are sent between devices in bfloat16 or wider.
A program may use at most 1 GiB of HBM per device.

v0:
```python
import jax
import jax.numpy as jnp
from jax import lax
from jax.sharding import PartitionSpec as P

ROW_CONTRACT = (((0,), (0,)), ((), ()))
COL_CONTRACT = (((1,), (1,)), ((), ()))


def solution(mesh):
    axis_name = 'nodes'

    def local_step(adj_rows, feat_rows, w_one, w_two, label_rows, mask_rows):
        weight_one = w_one.astype(jnp.bfloat16)
        weight_two = w_two.astype(jnp.bfloat16)
        num_classes = w_two.shape[1]
        feats_all = lax.all_gather(feat_rows, axis_name, tiled=True)
        agg_one = jnp.dot(adj_rows, feats_all, preferred_element_type=jnp.float32).astype(jnp.bfloat16)
        pre_one = jnp.dot(agg_one, weight_one, preferred_element_type=jnp.float32)
        hidden = jnp.maximum(pre_one, 0.0).astype(jnp.bfloat16)
        hidden_all = lax.all_gather(hidden, axis_name, tiled=True)
        agg_two = jnp.dot(adj_rows, hidden_all, preferred_element_type=jnp.float32).astype(jnp.bfloat16)
        logits = jnp.dot(agg_two, weight_two, preferred_element_type=jnp.float32)
        weight = mask_rows.astype(jnp.float32)
        label_count = lax.psum(jnp.sum(weight), axis_name)
        onehot = (label_rows[:, None] == jnp.arange(num_classes)[None, :]).astype(jnp.float32)
        log_prob = jax.nn.log_softmax(logits, axis=-1)
        loss_sum = lax.psum(-jnp.sum(weight * jnp.sum(onehot * log_prob, axis=-1)), axis_name)
        grad_two = (weight[:, None] * (jnp.exp(log_prob) - onehot) / label_count).astype(jnp.bfloat16)
        dw_two = lax.psum(lax.dot_general(agg_two, grad_two, ROW_CONTRACT, preferred_element_type=jnp.float32), axis_name)
        back_two = lax.dot_general(grad_two, weight_two, COL_CONTRACT, preferred_element_type=jnp.float32).astype(jnp.bfloat16)
        part_sums = lax.dot_general(adj_rows, back_two, ROW_CONTRACT, preferred_element_type=jnp.float32)
        d_hidden = lax.psum_scatter(part_sums, axis_name, scatter_dimension=0, tiled=True)
        grad_one = jnp.where(pre_one > 0.0, d_hidden, 0.0).astype(jnp.bfloat16)
        dw_one = lax.psum(lax.dot_general(agg_one, grad_one, ROW_CONTRACT, preferred_element_type=jnp.float32), axis_name)
        return ((loss_sum / label_count).reshape(1), dw_one, dw_two)

    return jax.shard_map(local_step, mesh=mesh, in_specs=(P(axis_name, None), P(axis_name, None), P(None, None), P(None, None), P(axis_name), P(axis_name)), out_specs=(P(None), P(None, None), P(None, None)), check_vma=False)
```

profile of v0, /device:TPU:0, one launch (start us, length us, event | category | flops | bytes accessed | tf_op | source)
XLA Modules:
  0.0 411.3 jit_solution(2985155843190279951)
XLA Ops:
  7.2 0.0 all-gather.3.cloned.1.call-start
  7.2 0.7 all-gather.3.cloned.1.call-update
  7.9 0.0 copy-start.1
  7.9 0.0 copy-start.3
  7.9 0.0 all-gather.5.cloned.1.call-start
  8.0 98.3 %all-gather.3.cloned.1.call-done = bf16[16384,602]{0,1:T(8,128)(2,1)} async-done(((bf16[1024,602]{0,1:T(8,128)(2,1)}), bf16[16384,602]{0,1:T(8,128)(2,1)}) %all-gather.3.cloned.1.call-update) | async-done | bytes 19726352 | tf_op jit(solution)/shard_map/all_gather | solution.py:17
  106.2 26.3 %convolution_convert_fusion = bf16[1024,602]{0,1:T(8,128)(2,1)S(1)} fusion(bf16[1024,16384]{1,0:T(8,128)(2,1)} %param.6, bf16[16384,602]{0,1:T(8,128)(2,1)} %all-gather.3.cloned.1.call-done), kind=kOutput, calls=%fused_computation.1 | convolution fusion | flops 20200384512 | bytes 54513664 | tf_op jit(solution)/shard_map/dot_general | solution.py:18
  132.6 0.0 copy-done.1
  132.6 1.3 maximum_convert_fusion
  133.9 0.0 all-gather.5.cloned.1.call-update
  133.9 0.0 reduce-scatter.2.cloned.1.call-start
  133.9 0.0 copy-done.3
  134.0 0.0 copy-start
  134.0 0.0 copy-start.2
  134.0 35.1 %all-gather.5.cloned.1.call-done = bf16[16384,128]{1,0:T(8,128)(2,1)} async-done(((bf16[1024,128]{1,0:T(8,128)(2,1)}), bf16[16384,128]{1,0:T(8,128)(2,1)}) %all-gather.5.cloned.1.call-update) | async-done | bytes 4194320 | tf_op jit(solution)/shard_map/all_gather | solution.py:21
  169.1 16.9 %convolution_convert_fusion.2 = bf16[128,1024]{1,0:T(8,128)(2,1)S(1)} fusion(bf16[16384,128]{1,0:T(8,128)(2,1)} %all-gather.5.cloned.1.call-done, bf16[1024,16384]{1,0:T(8,128)(2,1)} %param.6), kind=kOutput, calls=%fused_computation.3 | convolution fusion | flops 4295098368 | bytes 38010880 | tf_op jit(solution)/shard_map/dot_general | solution.py:22
  186.0 0.0 copy-done
  186.0 0.2 fusion.9
  186.2 0.0 copy-done.2
  186.3 0.6 convert_reduce_fusion
  186.9 32.1 %psum.29 = f32[]{:T(128)} all-reduce(f32[]{:T(128)} %get-tuple-element.3), channel_id=1, replica_groups=mesh['nodes'=16] {'nodes'}, use_global_device_ids=true, to_apply=%region_6.7 | all-reduce | flops 1 | bytes 8 | tf_op jit(solution)/shard_map/psum | solution.py:25
  219.0 0.7 divide_convert_fusion
  219.7 20.1 %convolution_bitcast_fusion = f32[16384,128]{1,0:T(8,128)} fusion(bf16[1024,16384]{1,0:T(8,128)(2,1)} %param.6, bf16[1024,41]{0,1:T(8,128)(2,1)S(1)} %divide_convert_fusion, f32[128,41]{0,1:T(8,128)S(1)} %copy-done), kind=kOutput, calls=%fused_computation | convolution fusion | flops 4305851392 | bytes 42048000 | tf_op jit(solution)/shard_map/dot_general | solution.py:32
  239.8 0.0 reduce-scatter.2.cloned.1.call-update
  239.8 0.0 all-reduce.3.cloned.1.call-start
  239.9 93.7 %reduce-scatter.2.cloned.1.call-done = f32[1024,128]{1,0:T(8,128)} async-done(((f32[16384,128]{1,0:T(8,128)}), f32[1024,128]{1,0:T(8,128)}) %reduce-scatter.2.cloned.1.call-update) | async-done | bytes 524304 | tf_op jit(solution)/shard_map/reduce_scatter | solution.py:33
  333.6 2.3 fusion
  335.8 0.0 all-reduce.3.cloned.1.call-update
  335.8 0.2 fusion.10
  336.7 31.7 %all-reduce = (f32[]{:T(128)}, f32[128,41]{0,1:T(8,128)}) all-reduce(f32[]{:T(128)S(6)} %neg.3, f32[128,41]{0,1:T(8,128)S(1)} %fusion.10), channel_id=1, replica_groups=mesh['nodes'=16] {'nodes'}, use_global_device_ids=true, to_apply=%region_4.5 | all-reduce | flops 5249 | bytes 41992 | tf_op jit(solution)/shard_map/psum | solution.py:28
  369.8 32.1 %all-reduce.3.cloned.1.call-done = f32[602,128]{1,0:T(8,128)} async-done(((f32[602,128]{1,0:T(8,128)}), f32[602,128]{1,0:T(8,128)}) %all-reduce.3.cloned.1.call-update) | async-done | bytes 308240 | tf_op jit(solution)/shard_map/psum | solution.py:35
  401.9 1.7 copy.10
  (4 shorter events, 0.1 us)
Async XLA Ops:
  7.2 99.1 %all-gather.3.cloned.1.call-start = ((), (), s32[]{:S(2)}) async-start(), calls=%async_computation.1 | async-start | bytes 21168128 | tf_op jit(solution)/shard_map/all_gather | solution.py:17
  7.9 124.7 %copy-start.1 = (f32[602,128]{1,0:T(8,128)S(1)}, f32[602,128]{1,0:T(8,128)}, u32[]{:S(2)}) copy-start(f32[602,128]{1,0:T(8,128)} %param.8) | copy-start | bytes 924676
  7.9 126.0 %copy-start.3 = (s32[1024]{0:T(1024)S(1)}, s32[1024]{0:T(1024)}, u32[]{:S(2)}) copy-start(s32[1024]{0:T(1024)} %param.11) | copy-start | bytes 12292
  7.9 161.1 %all-gather.5.cloned.1.call-start = ((), (), s32[]{:S(2)}) async-start(), calls=%async_computation.2 | async-start | bytes 4456448 | tf_op jit(solution)/shard_map/all_gather | solution.py:21
  133.9 199.7 %reduce-scatter.2.cloned.1.call-start = ((), (), s32[]{:S(2)}) async-start(), calls=%async_computation.3 | async-start | bytes 8912896 | tf_op jit(solution)/shard_map/reduce_scatter | solution.py:33
  134.0 52.0 %copy-start = (f32[128,41]{0,1:T(8,128)S(1)}, f32[128,41]{0,1:T(8,128)}, u32[]{:S(2)}) copy-start(f32[128,41]{0,1:T(8,128)} %param.9) | copy-start | bytes 62980
  134.0 52.2 %copy-start.2 = (s32[1024]{0:T(1024)S(1)}, s32[1024]{0:T(1024)}, u32[]{:S(2)}) copy-start(s32[1024]{0:T(1024)} %param.10) | copy-start | bytes 12292
  239.8 162.1 %all-reduce.3.cloned.1.call-start = ((), (), s32[]{:S(2)}) async-start(), calls=%async_computation.4 | async-start | bytes 622592 | tf_op jit(solution)/shard_map/psum | solution.py:35
Sparse Core Ops, SparseCore 0:
  10.2 95.9 all-gather.2
  134.0 35.0 all-gather.4
  239.9 93.5 reduce-scatter.1
  338.2 63.6 all-reduce.2
where the time goes:
time: 412 us; the launch traced here: 411 us
  waiting for transfers between devices  260 us (63%)
  matrix products  67.2 us (16%)
  blocking collectives  63.8 us (15%)
  between operations  17.1 us (4%)
    all_gather x1, waiting for transfers between devices, local_step(): feats_all = lax.all_gather(feat_rows, axis_name, tiled=True)  98.3 us
    reduce_scatter x1, waiting for transfers between devices, local_step(): lax.psum_scatter(part_sums, axis_name, scatter_dimension=0, tiled=True)  93.7 us
    all_gather x1, waiting for transfers between devices, local_step(): hidden_all = lax.all_gather(hidden, axis_name, tiled=True)  35.1 us
    psum x1, waiting for transfers between devices, local_step(): lax.psum(lax.dot_general(agg_one, grad_one, ROW_CONTRACT, preferred_eleme...  32.1 us
    psum x1, blocking collectives, local_step(): label_count = lax.psum(jnp.sum(weight), axis_name)  32.1 us
    psum x1, blocking collectives, local_step(): lax.psum(-jnp.sum(weight * jnp.sum(onehot * log_prob, axis=-1)), axis_name)  31.7 us
    dot_general x1, matrix products, local_step(): jnp.dot(adj_rows, feats_all, preferred_element_type=jnp.float32)  26.3 us
    dot_general x1, matrix products, local_step(): lax.dot_general(adj_rows, back_two, ROW_CONTRACT, preferred_element_type=...  20.1 us
  transfers between devices with their start and end apart: 4, of which 4 were waited for; matrix products, arithmetic and copies ran while one was open for 0% of the time, Pallas kernels for 0%

commit v1 on v0

v1 whole, which is shorter than its diff:
```python
import functools

import jax
import jax.numpy as jnp
from jax import lax
from jax.experimental import pallas as pl
from jax.experimental.pallas import tpu as pltpu
from jax.sharding import PartitionSpec as P

MESH = pl.DeviceIdType.MESH
AXIS = 'nodes'
TREES = 4
STEPS = 8
ROW_CONTRACT = (((0,), (0,)), ((), ()))
COL_CONTRACT = (((1,), (1,)), ((), ()))


def tree_axis(tree, k, core, chip):
    if tree < 3:
        weight = 2 ** ((tree + k) % 3)
        return weight, lax.rem(chip // weight, 2)
    weight = (1 - core) * 2 ** k + core * 2 ** (2 - k)
    low, high = lax.rem(chip // 2 ** k, 2), lax.rem(chip // 2 ** (2 - k), 2)
    return weight, (1 - core) * low + core * high


def chip_at(tree, offset, core, chip):
    out = chip
    for k in range(3):
        weight, bit = tree_axis(tree, k, core, chip)
        out = out + lax.rem(offset // 2 ** k, 2) * weight * (1 - 2 * bit)
    return out


def unit_at(tree, offset, core, chip):
    return (chip_at(tree, offset, core, chip) * 2 + core) * TREES + tree


def neighbour(tree, k, core, chip):
    weight, bit = tree_axis(tree, k, core, chip)
    return (chip + weight * (1 - 2 * bit)) * 2 + core


def remote(src, dst, send_sem, recv_sem, device):
    return pltpu.make_async_remote_copy(src_ref=src, dst_ref=dst, send_sem=send_sem, recv_sem=recv_sem, device_id=(device,), device_id_type=MESH)


def place():
    me = lax.axis_index(AXIS)
    core, chip = lax.rem(me, 2), me // 2
    return me, core, chip, chip * 2 + 1 - core


def gather_start(own, buf, sems):
    send, recv, dsend, drecv = sems
    me, core, chip, partner = place()
    for k in range(3):
        for t in range(TREES):
            u = me * TREES + t
            remote(own.at[t], buf.at[u], send.at[0, t, k], recv.at[2 ** k, t], neighbour(t, k, core, chip)).start()
    for t in range(TREES):
        u = me * TREES + t
        remote(own.at[t], buf.at[u], dsend.at[0, t], drecv.at[0, t], partner).start()


def gather_loop(own, buf, sems, consume):
    send, recv, dsend, drecv = sems
    me, core, chip, partner = place()

    def step(s, carry):
        for t in range(TREES):
            u = unit_at(t, s, core, chip)

            @pl.when(s > 0)
            def _():
                remote(own.at[t], buf.at[u], send.at[0, t, 0], recv.at[s, t], partner).wait_recv()
                for k in range(1, 3):
                    @pl.when(s < 2 ** k)
                    def _():
                        remote(buf.at[u], buf.at[u], send.at[s, t, k], recv.at[s + 2 ** k, t], neighbour(t, k, core, chip)).start()
                remote(buf.at[u], buf.at[u], dsend.at[s, t], drecv.at[s, t], partner).start()
        for t in range(TREES):
            other = unit_at(t, s, 1 - core, chip)
            remote(own.at[t], buf.at[other], dsend.at[0, t], drecv.at[s, t], partner).wait_recv()
            consume(unit_at(t, s, core, chip), other)
        return carry

    lax.fori_loop(0, STEPS, step, 0)


def gather_drain(own, buf, sems):
    send, recv, dsend, drecv = sems
    me, core, chip, partner = place()

    def step(s, carry):
        for t in range(TREES):
            for k in range(3):
                @pl.when(s < 2 ** k)
                def _():
                    remote(own.at[t], buf.at[0], send.at[s, t, k], recv.at[0, t], partner).wait_send()
            remote(own.at[t], buf.at[0], dsend.at[s, t], drecv.at[0, t], partner).wait_send()
        return carry

    lax.fori_loop(0, STEPS, step, 0)


def gather_sems():
    dma = pltpu.SemaphoreType.DMA
    return [dma((4, TREES, 3)), dma((STEPS, TREES)), dma((STEPS, TREES)), dma((STEPS, TREES))]


def barrier_near():
    me, core, chip, partner = place()
    sem = pltpu.get_barrier_semaphore()
    pl.semaphore_signal(sem, inc=1, device_id=(partner,), device_id_type=MESH)
    for k in range(3):
        pl.semaphore_signal(sem, inc=1, device_id=(neighbour(0, k, core, chip),), device_id_type=MESH)
    pl.semaphore_wait(sem, 4)


def load_adj(adj, adj_v, sems):
    blocks = sems.shape[0]
    width = adj.shape[1] // blocks
    return [pltpu.make_async_copy(adj.at[:, pl.ds(b * width, width)], adj_v.at[:, pl.ds(b * width, width)], sems.at[b]) for b in range(blocks)]


def layer_one_kernel(x_ref, w_ref, adj, s_ref, z_ref, h_ref, adj_v, buf, acc, adj_sem, *sems):
    me, core, chip, partner = place()
    loads = load_adj(adj, adj_v, adj_sem)
    for copy in loads:
        copy.start()
    barrier_near()
    gather_start(x_ref, buf, sems)
    width = x_ref.shape[2]
    for t in range(TREES):
        buf[me * TREES + t] = x_ref[t]
    acc[...] = jnp.zeros_like(acc)
    for copy in loads:
        copy.wait()

    def term(u):
        cols = pl.ds(pl.multiple_of(u * width, width), width)
        return lax.dot_general(buf[u], adj_v[:, cols], COL_CONTRACT, preferred_element_type=jnp.float32)

    def consume(mine, other):
        acc[...] += term(mine) + term(other)

    gather_loop(x_ref, buf, sems, consume)
    s_ref[...] = acc[...].astype(jnp.bfloat16)
    z = jnp.dot(w_ref[...], s_ref[...], preferred_element_type=jnp.float32)
    z_ref[...] = z
    h_ref[...] = jnp.maximum(z, 0.0).astype(jnp.bfloat16)
    gather_drain(x_ref, buf, sems)


def layer_one(x_units, w_rows, adj):
    rows, nodes = adj.shape
    units, feats, width = nodes // x_units.shape[2], x_units.shape[1], x_units.shape[2]
    hidden = w_rows.shape[0]
    vmem = pl.BlockSpec(memory_space=pltpu.VMEM)
    return pl.pallas_call(
        layer_one_kernel,
        name='layer_one',
        out_shape=(jax.ShapeDtypeStruct((feats, rows), jnp.bfloat16), jax.ShapeDtypeStruct((hidden, rows), jnp.float32), jax.ShapeDtypeStruct((hidden, rows), jnp.bfloat16)),
        in_specs=[vmem, vmem, pl.BlockSpec(memory_space=pl.ANY)],
        out_specs=(vmem, vmem, vmem),
        scratch_shapes=[pltpu.VMEM((rows, nodes), jnp.bfloat16), pltpu.VMEM((units, feats, width), jnp.bfloat16), pltpu.VMEM((feats, rows), jnp.float32), pltpu.SemaphoreType.DMA((16,)), *gather_sems()],
        compiler_params=pltpu.CompilerParams(collective_id=0, has_side_effects=True, vmem_limit_bytes=67043328),
        cost_estimate=pl.CostEstimate(flops=2 * rows * nodes * feats, bytes_accessed=2 * rows * nodes, transcendentals=0),
    )(x_units, w_rows, adj)


def solution(mesh):
    axis_name = AXIS

    def local_step(adj_rows, feat_rows, w_one, w_two, label_rows, mask_rows):
        rows, feats = feat_rows.shape
        padded = -(-feats // 16) * 16
        width = rows // TREES
        x_units = jnp.pad(feat_rows.reshape(TREES, width, feats).transpose(0, 2, 1), ((0, 0), (0, padded - feats), (0, 0)))
        w_rows = jnp.pad(w_one.T, ((0, 0), (0, padded - feats))).astype(jnp.bfloat16)
        agg_one, pre_one, hidden = layer_one(x_units, w_rows, adj_rows)
        weight_two = w_two.astype(jnp.bfloat16)
        num_classes = w_two.shape[1]
        hidden_all = lax.all_gather(hidden, axis_name, tiled=True, axis=1)
        agg_two = lax.dot_general(adj_rows, hidden_all, COL_CONTRACT, preferred_element_type=jnp.float32).astype(jnp.bfloat16)
        logits = jnp.dot(agg_two, weight_two, preferred_element_type=jnp.float32)
        weight = mask_rows.astype(jnp.float32)
        label_count = lax.psum(jnp.sum(weight), axis_name)
        onehot = (label_rows[:, None] == jnp.arange(num_classes)[None, :]).astype(jnp.float32)
        log_prob = jax.nn.log_softmax(logits, axis=-1)
        loss_sum = lax.psum(-jnp.sum(weight * jnp.sum(onehot * log_prob, axis=-1)), axis_name)
        grad_two = (weight[:, None] * (jnp.exp(log_prob) - onehot) / label_count).astype(jnp.bfloat16)
        dw_two = lax.psum(lax.dot_general(agg_two, grad_two, ROW_CONTRACT, preferred_element_type=jnp.float32), axis_name)
        back_two = lax.dot_general(grad_two, weight_two, COL_CONTRACT, preferred_element_type=jnp.float32).astype(jnp.bfloat16)
        part_sums = lax.dot_general(adj_rows, back_two, ROW_CONTRACT, preferred_element_type=jnp.float32)
        d_hidden = lax.psum_scatter(part_sums, axis_name, scatter_dimension=0, tiled=True)
        grad_one = jnp.where(pre_one.T > 0.0, d_hidden, 0.0).astype(jnp.bfloat16)
        dw_one = lax.psum(lax.dot_general(agg_one, grad_one, (((1,), (0,)), ((), ())), preferred_element_type=jnp.float32), axis_name)[:feats]
        return ((loss_sum / label_count).reshape(1), dw_one, dw_two)

    return jax.shard_map(local_step, mesh=mesh, in_specs=(P(axis_name, None), P(axis_name, None), P(None, None), P(None, None), P(axis_name), P(axis_name)), out_specs=(P(None), P(None, None), P(None, None)), check_vma=False)
```

time: 412 us -> 368 us (0.89)
  waiting for transfers between devices: 260 us -> 162 us
  Pallas kernels: 0 us -> 79.7 us
  matrix products: 67.2 us -> 35.9 us
  local copies, waits for them, and re-layouts: 1.73 us -> 6.03 us
    all_gather x2 -> x1, waiting for transfers between devices: 133 us -> 35.8 us  [local_step(): hidden_all = lax.all_gather(hidden, axis_name, tiled=True, axis=1)]
    pallas_call x0 -> x1, Pallas kernels: none -> 79.7 us  [layer_one(): pl.pallas_call(layer_one_kernel, name='layer_one', out_shape=(jax.ShapeDt...]
    dot_general x4 -> x2, matrix products: 46.7 us -> 18.8 us  [the longest x1 16.6 us: local_step(): lax.dot_general(adj_rows, hidden_all, COL_CONTRACT, preferred_element_typ...]
  transfers between devices with their start and end apart: 4 -> 3, of which waited for: 4 -> 3; matrix products, arithmetic and copies ran while one was open for 0% -> 0% of each run, Pallas kernels for 0% -> 0%
where the time goes in v1:
time: 368 us; the launch traced here: 367 us
  waiting for transfers between devices  162 us (44%)
  Pallas kernels  79.7 us (22%)
  blocking collectives  63.6 us (17%)
  matrix products  35.9 us (10%)
  between operations  17 us (5%)
  local copies, waits for them, and re-layouts  6.03 us (2%)
    reduce_scatter x1, waiting for transfers between devices, local_step(): lax.psum_scatter(part_sums, axis_name, scatter_dimension=0, tiled=True)  93.7 us
    pallas_call x1, Pallas kernels, layer_one(): pl.pallas_call(layer_one_kernel, name='layer_one', out_shape=(jax.ShapeDt...  79.7 us
    all_gather x1, waiting for transfers between devices, local_step(): hidden_all = lax.all_gather(hidden, axis_name, tiled=True, axis=1)  35.8 us
    psum x1, waiting for transfers between devices, local_step(): lax.psum(lax.dot_general(agg_one, grad_one, (((1,), (0,)), ((), ())), pre...  32.3 us
    psum x1, blocking collectives, local_step(): label_count = lax.psum(jnp.sum(weight), axis_name)  31.9 us
    psum x1, blocking collectives, local_step(): lax.psum(-jnp.sum(weight * jnp.sum(onehot * log_prob, axis=-1)), axis_name)  31.7 us
    dot_general x1, matrix products, local_step(): lax.dot_general(adj_rows, back_two, ROW_CONTRACT, preferred_element_type=...  16.7 us
    dot_general x1, matrix products, local_step(): lax.dot_general(adj_rows, hidden_all, COL_CONTRACT, preferred_element_typ...  16.6 us
  transfers between devices with their start and end apart: 3, of which 3 were waited for; matrix products, arithmetic and copies ran while one was open for 0% of the time, Pallas kernels for 0%

profile of v1, /device:TPU:0, one launch (start us, length us, event | category | flops | bytes accessed | tf_op | source)
XLA Modules:
  0.0 367.3 jit_solution(8952315784598140610)
XLA Ops:
  7.2 0.0 all-gather.2.cloned.1.call-start
  7.2 1.0 convert.5
  8.2 0.2 copy.15
  8.4 1.7 copy.13
  10.1 0.6 copy.14
  10.7 0.7 pad.10.w_ref
  11.4 1.1 pad.9.x_ref
  12.5 79.7 %layer_one.1 = (bf16[608,1024]{1,0:T(8,128)(2,1)}, f32[128,1024]{1,0:T(8,128)}, bf16[128,1024]{1,0:T(8,128)(2,1)}) custom-call(bf16[4,608,256]{2,1,0:T(8,128)(2,1)} %pad.9.x_ref, bf16[128,608]{1,0:T(8,128)(2,1)} %pad.10.w_ref, bf16[1024,16384]{1,0:T(8,128)(2,1)} %adj.1), custom_call_target="tpu_custom_call" | custom-call | flops 20401094656 | bytes 33554432 | tf_op jit(solution)/shard_map/layer_one/pallas_call | solution.py:161
  92.2 0.0 all-gather.2.cloned.1.call-update
  92.2 0.0 reduce-scatter.2.cloned.1.call-start
  92.3 0.7 convert_element_type.27
  93.0 0.0 copy-start.2
  93.0 0.0 copy-start.3
  93.0 0.0 copy-start.4
  93.0 35.8 %all-gather.2.cloned.1.call-done = bf16[128,16384]{1,0:T(8,128)(2,1)} async-done(((bf16[128,1024]{1,0:T(8,128)(2,1)}), bf16[128,16384]{1,0:T(8,128)(2,1)}) %all-gather.2.cloned.1.call-update) | async-done | bytes 4194320 | tf_op jit(solution)/shard_map/all_gather | solution.py:185
  128.8 16.6 %convolution_convert_fusion.1 = bf16[128,1024]{1,0:T(8,128)(2,1)S(1)} fusion(bf16[128,16384]{1,0:T(8,128)(2,1)} %all-gather.2.cloned.1.call-done, bf16[1024,16384]{1,0:T(8,128)(2,1)} %adj.1), kind=kOutput, calls=%fused_computation.2 | convolution fusion | flops 4295098368 | bytes 38010880 | tf_op jit(solution)/shard_map/dot_general | solution.py:186
  145.4 0.0 copy-done.2
  145.4 0.2 fusion.8
  145.6 0.0 copy-done.3
  145.7 0.0 copy-done.4
  145.7 0.6 convert_reduce_fusion
  146.3 31.9 %psum.29 = f32[]{:T(128)} all-reduce(f32[]{:T(128)} %get-tuple-element.9), channel_id=1, replica_groups=mesh['nodes'=16] {'nodes'}, use_global_device_ids=true, to_apply=%region_6.7 | all-reduce | flops 1 | bytes 8 | tf_op jit(solution)/shard_map/psum | solution.py:189
  178.2 0.7 divide_convert_fusion
  178.9 16.7 %convolution_bitcast_fusion = f32[16384,128]{0,1:T(8,128)} fusion(bf16[1024,16384]{1,0:T(8,128)(2,1)} %adj.1, bf16[1024,41]{0,1:T(8,128)(2,1)S(1)} %divide_convert_fusion, f32[128,41]{0,1:T(8,128)S(1)} %copy-done.2), kind=kOutput, calls=%fused_computation | convolution fusion | flops 4305851392 | bytes 42048000 | tf_op jit(solution)/shard_map/dot_general | solution.py:196
  195.7 0.0 copy-start
  195.7 0.0 copy-start.1
  195.7 0.0 reduce-scatter.2.cloned.1.call-update
  195.7 0.0 all-reduce.5.cloned.1.call-start
  195.7 93.7 %reduce-scatter.2.cloned.1.call-done = f32[1024,128]{0,1:T(8,128)} async-done(((f32[16384,128]{0,1:T(8,128)}), f32[1024,128]{0,1:T(8,128)}) %reduce-scatter.2.cloned.1.call-update) | async-done | bytes 524304 | tf_op jit(solution)/shard_map/reduce_scatter | solution.py:197
  289.4 0.0 copy-done
  289.4 0.0 copy-done.1
  289.4 2.3 fusion
  291.7 0.0 all-reduce.5.cloned.1.call-update
  291.7 0.2 fusion.9
  292.6 31.7 %all-reduce.2 = (f32[]{:T(128)}, f32[128,41]{0,1:T(8,128)}) all-reduce(f32[]{:T(128)S(6)} %neg.3, f32[128,41]{0,1:T(8,128)S(1)} %fusion.9), channel_id=1, replica_groups=mesh['nodes'=16] {'nodes'}, use_global_device_ids=true, to_apply=%region_4.5 | all-reduce | flops 5249 | bytes 41992 | tf_op jit(solution)/shard_map/psum | solution.py:192
  325.6 32.3 %all-reduce.5.cloned.1.call-done = f32[608,128]{1,0:T(8,128)} async-done(((f32[608,128]{1,0:T(8,128)}), f32[608,128]{1,0:T(8,128)}) %all-reduce.5.cloned.1.call-update) | async-done | bytes 311312 | tf_op jit(solution)/shard_map/psum | solution.py:199
  357.9 1.7 copy.17
  (3 shorter events, 0.1 us)
Async XLA Ops:
  7.2 121.6 %all-gather.2.cloned.1.call-start = ((), (), s32[]{:S(2)}) async-start(), calls=%async_computation.1 | async-start | bytes 4456448 | tf_op jit(solution)/shard_map/all_gather | solution.py:185
  92.2 197.2 %reduce-scatter.2.cloned.1.call-start = ((), (), s32[]{:S(2)}) async-start(), calls=%async_computation.2 | async-start | bytes 8912896 | tf_op jit(solution)/shard_map/reduce_scatter | solution.py:197
  93.0 52.4 %copy-start.2 = (f32[128,41]{0,1:T(8,128)S(1)}, f32[128,41]{0,1:T(8,128)}, u32[]{:S(2)}) copy-start(f32[128,41]{0,1:T(8,128)} %param.9) | copy-start | bytes 62980
  93.0 52.7 %copy-start.3 = (s32[1024]{0:T(1024)S(1)}, s32[1024]{0:T(1024)}, u32[]{:S(2)}) copy-start(s32[1024]{0:T(1024)} %param.10) | copy-start | bytes 12292
  93.0 52.7 %copy-start.4 = (s32[1024]{0:T(1024)S(1)}, s32[1024]{0:T(1024)}, u32[]{:S(2)}) copy-start(s32[1024]{0:T(1024)} %param.11) | copy-start | bytes 12292
  195.7 93.8 %copy-start = (bf16[608,1024]{1,0:T(8,128)(2,1)S(1)}, bf16[608,1024]{1,0:T(8,128)(2,1)}, u32[]{:S(2)}) copy-start(bf16[608,1024]{1,0:T(8,128)(2,1)} %get-tuple-element.7) | copy-start | bytes 3735556
  195.7 93.8 %copy-start.1 = (f32[128,1024]{1,0:T(8,128)S(1)}, f32[128,1024]{1,0:T(8,128)}, u32[]{:S(2)}) copy-start(f32[128,1024]{1,0:T(8,128)} %get-tuple-element.8) | copy-start | bytes 1572868
  195.7 162.2 %all-reduce.5.cloned.1.call-start = ((), (), s32[]{:S(2)}) async-start(), calls=%async_computation.3 | async-start | bytes 622592 | tf_op jit(solution)/shard_map/psum | solution.py:199
Sparse Core Ops, SparseCore 0:
  92.4 36.3 all-gather.1
  195.8 93.5 reduce-scatter.1
  294.2 63.6 all-reduce.4

commit v2 on v1

v2 whole, which is shorter than its diff:
```python
import functools

import jax
import jax.numpy as jnp
from jax import lax
from jax.experimental import pallas as pl
from jax.experimental.pallas import tpu as pltpu
from jax.sharding import PartitionSpec as P

MESH = pl.DeviceIdType.MESH
AXIS = 'nodes'
TREES = 4
STEPS = 8
COL_CONTRACT = (((1,), (1,)), ((), ()))
ROW_CONTRACT = (((0,), (0,)), ((), ()))


def tree_axis(tree, k, core, chip):
    if tree < 3:
        weight = 2 ** ((tree + k) % 3)
        return weight, lax.rem(chip // weight, 2)
    weight = (1 - core) * 2 ** k + core * 2 ** (2 - k)
    low, high = lax.rem(chip // 2 ** k, 2), lax.rem(chip // 2 ** (2 - k), 2)
    return weight, (1 - core) * low + core * high


def chip_at(tree, offset, core, chip):
    out = chip
    for k in range(3):
        weight, bit = tree_axis(tree, k, core, chip)
        out = out + lax.rem(offset // 2 ** k, 2) * weight * (1 - 2 * bit)
    return out


def unit_at(tree, offset, core, chip):
    return (chip_at(tree, offset, core, chip) * 2 + core) * TREES + tree


def neighbour(tree, k, core, chip):
    weight, bit = tree_axis(tree, k, core, chip)
    return (chip + weight * (1 - 2 * bit)) * 2 + core


def remote(src, dst, send_sem, recv_sem, device):
    return pltpu.make_async_remote_copy(src_ref=src, dst_ref=dst, send_sem=send_sem, recv_sem=recv_sem, device_id=(device,), device_id_type=MESH)


def place():
    me = lax.axis_index(AXIS)
    core, chip = lax.rem(me, 2), me // 2
    return me, core, chip, chip * 2 + 1 - core


def gather_start(buf, sems):
    send, recv, dsend, drecv = sems
    me, core, chip, partner = place()
    for k in range(3):
        for t in range(TREES):
            u = me * TREES + t
            remote(buf.at[u], buf.at[u], send.at[0, t, k], recv.at[2 ** k, t], neighbour(t, k, core, chip)).start()
    for t in range(TREES):
        u = me * TREES + t
        remote(buf.at[u], buf.at[u], dsend.at[0, t], drecv.at[0, t], partner).start()


def gather_loop(buf, sems, consume):
    send, recv, dsend, drecv = sems
    me, core, chip, partner = place()

    def step(s, carry):
        for t in range(TREES):
            u = unit_at(t, s, core, chip)

            @pl.when(s > 0)
            def _():
                remote(buf.at[u], buf.at[u], send.at[0, t, 0], recv.at[s, t], partner).wait_recv()
                for k in range(1, 3):
                    @pl.when(s < 2 ** k)
                    def _():
                        remote(buf.at[u], buf.at[u], send.at[s, t, k], recv.at[s + 2 ** k, t], neighbour(t, k, core, chip)).start()
                remote(buf.at[u], buf.at[u], dsend.at[s, t], drecv.at[s, t], partner).start()
        for t in range(TREES):
            other = unit_at(t, s, 1 - core, chip)
            remote(buf.at[other], buf.at[other], dsend.at[0, t], drecv.at[s, t], partner).wait_recv()
            consume(unit_at(t, s, core, chip), other)
        return carry

    lax.fori_loop(0, STEPS, step, 0)


def gather_drain(buf, sems):
    send, recv, dsend, drecv = sems
    me, core, chip, partner = place()

    def step(s, carry):
        for t in range(TREES):
            for k in range(3):
                @pl.when(s < 2 ** k)
                def _():
                    remote(buf.at[0], buf.at[0], send.at[s, t, k], recv.at[0, t], partner).wait_send()
            remote(buf.at[0], buf.at[0], dsend.at[s, t], drecv.at[0, t], partner).wait_send()
        return carry

    lax.fori_loop(0, STEPS, step, 0)


def gather_sems():
    dma = pltpu.SemaphoreType.DMA
    return [dma((4, TREES, 3)), dma((STEPS, TREES)), dma((STEPS, TREES)), dma((STEPS, TREES))]


def barrier_all(n):
    me = lax.axis_index(AXIS)
    sem = pltpu.get_barrier_semaphore()
    for i in range(1, n):
        pl.semaphore_signal(sem, inc=1, device_id=(lax.rem(me + i, n),), device_id_type=MESH)
    pl.semaphore_wait(sem, n - 1)


def send_all(n, src, dst, send_sem, recv_sem):
    me = lax.axis_index(AXIS)
    for i in range(1, n):
        to = lax.rem(me + i, n)
        remote(src(to), dst, send_sem.at[i], recv_sem.at[i], to).start()


def wait_all(n, src, dst, send_sem, recv_sem):
    me = lax.axis_index(AXIS)
    for i in range(1, n):
        to = lax.rem(me + i, n)
        copy = remote(src(to), dst, send_sem.at[i], recv_sem.at[i], to)
        copy.wait_send()
        copy.wait_recv()


def forward_kernel(n, x_ref, w_ref, w2t_ref, y_ref, m_ref, adj, s_ref, z_ref, u_ref, small_ref,
                   adj_v, buf, acc, h_buf, count, adj_sem, x_sem, count_send, count_recv, *sems):
    me, core, chip, partner = place()
    sems_x, sems_h = sems[:4], sems[4:]
    width = buf.shape[2]
    hidden = h_buf.shape[1]
    fetch = [pltpu.make_async_copy(x_ref.at[:, pl.ds(t * width, width)], buf.at[me * TREES + t], x_sem.at[t]) for t in range(TREES)]
    for copy in fetch:
        copy.start()
    blocks = adj_sem.shape[0]
    block = adj.shape[1] // blocks
    loads = [pltpu.make_async_copy(adj.at[:, pl.ds(b * block, block)], adj_v.at[:, pl.ds(b * block, block)], adj_sem.at[b]) for b in range(blocks)]
    for copy in loads:
        copy.start()
    weight = m_ref[...].astype(jnp.float32)
    count[me] = jnp.broadcast_to(jnp.sum(weight, axis=1, keepdims=True), count.shape[1:])
    barrier_all(n)
    for copy in fetch:
        copy.wait()
    gather_start(buf, sems_x)
    send_all(n, lambda to: count.at[me], count.at[me], count_send, count_recv)
    acc[...] = jnp.zeros_like(acc)
    for copy in loads:
        copy.wait()

    def term(units, u):
        cols = pl.ds(pl.multiple_of(u * width, width), width)
        return lax.dot_general(units[u], adj_v[:, cols], COL_CONTRACT, preferred_element_type=jnp.float32)

    def consume_one(mine, other):
        acc[...] += term(buf, mine) + term(buf, other)

    def consume_two(mine, other):
        acc[0:hidden] += term(h_buf, mine) + term(h_buf, other)

    gather_loop(buf, sems_x, consume_one)
    s_ref[...] = acc[...].astype(jnp.bfloat16)
    w_rows = w_ref[...].astype(jnp.bfloat16)
    for t in range(TREES):
        cols = slice(t * width, (t + 1) * width)
        z = lax.dot_general(w_rows, s_ref[:, cols], ROW_CONTRACT, preferred_element_type=jnp.float32)
        z_ref[:, cols] = z
        h_buf[me * TREES + t] = jnp.maximum(z, 0.0).astype(jnp.bfloat16)
    gather_start(h_buf, sems_h)
    acc[0:hidden] = jnp.zeros_like(acc[0:hidden])
    gather_drain(buf, sems_x)
    wait_all(n, lambda to: count.at[me], count.at[me], count_send, count_recv)
    total = jnp.sum(count[...], axis=0)[0:1, 0:1]
    gather_loop(h_buf, sems_h, consume_two)

    s_two = acc[0:hidden].astype(jnp.bfloat16)
    w_two = w2t_ref[...].astype(jnp.bfloat16)
    logits = jnp.dot(w_two, s_two, preferred_element_type=jnp.float32)
    shifted = logits - jnp.max(logits, axis=0, keepdims=True)
    log_prob = shifted - jnp.log(jnp.sum(jnp.exp(shifted), axis=0, keepdims=True))
    hot = lax.broadcasted_iota(jnp.int32, logits.shape, 0) == y_ref[...]
    loss = -jnp.sum(weight * jnp.sum(jnp.where(hot, log_prob, 0.0), axis=0, keepdims=True), axis=1, keepdims=True)
    grad = (weight * (jnp.exp(log_prob) - hot.astype(jnp.float32)) / total).astype(jnp.bfloat16)
    u_ref[...] = lax.dot_general(w_two, grad, ROW_CONTRACT, preferred_element_type=jnp.float32).astype(jnp.bfloat16)
    classes = logits.shape[0]
    edge = small_ref.shape[0] - 8
    small_ref[0:classes] = lax.dot_general(grad, s_two, COL_CONTRACT, preferred_element_type=jnp.float32)
    small_ref[classes:edge] = jnp.zeros((edge - classes, hidden), jnp.float32)
    small_ref[edge:] = jnp.broadcast_to(loss / total, (8, hidden))
    gather_drain(h_buf, sems_h)


def forward(x_rows, w_one, w2t, labels, mask, adj):
    rows, nodes = adj.shape
    n = nodes // rows
    feats, width = x_rows.shape[0], rows // TREES
    classes, hidden = w2t.shape
    units = n * TREES
    edge = -(-classes // 8) * 8 + 8
    vmem, hbm = pl.BlockSpec(memory_space=pltpu.VMEM), pl.BlockSpec(memory_space=pl.ANY)
    dma = pltpu.SemaphoreType.DMA
    return pl.pallas_call(
        functools.partial(forward_kernel, n),
        name='forward',
        out_shape=(jax.ShapeDtypeStruct((feats, rows), jnp.bfloat16), jax.ShapeDtypeStruct((hidden, rows), jnp.float32),
                   jax.ShapeDtypeStruct((hidden, rows), jnp.bfloat16), jax.ShapeDtypeStruct((edge, hidden), jnp.float32)),
        in_specs=[hbm] + [vmem] * 4 + [hbm],
        out_specs=(vmem,) * 4,
        scratch_shapes=[
            pltpu.VMEM((rows, nodes), jnp.bfloat16), pltpu.VMEM((units, feats, width), jnp.bfloat16), pltpu.VMEM((feats, rows), jnp.float32),
            pltpu.VMEM((units, hidden, width), jnp.bfloat16), pltpu.VMEM((n, 8, 128), jnp.float32),
            dma((16,)), dma((TREES,)), dma((n,)), dma((n,)), *gather_sems(), *gather_sems()],
        compiler_params=pltpu.CompilerParams(collective_id=0, has_side_effects=True, vmem_limit_bytes=67043328),
        cost_estimate=pl.CostEstimate(flops=2 * rows * nodes * (feats + hidden), bytes_accessed=2 * rows * nodes, transcendentals=0),
    )(x_rows, w_one, w2t, labels, mask, adj)


def backward_kernel(n, u_ref, s_ref, z_ref, small_ref, adj, loss_ref, dw_ref, dw2_ref,
                    adj_v, stage, total, child, part, parts, whole, adj_sem, dsend, drecv, csend, crecv, fsend, frecv, gsend, grecv):
    me, core, chip, partner = place()
    width = adj_v.shape[2]

    def load(s, t, side):
        which = core + side - 2 * core * side
        u = unit_at(t, s, which, chip)
        cols = pl.ds(pl.multiple_of(u * width, width), width)
        return pltpu.make_async_copy(adj.at[:, cols], adj_v.at[(s * TREES + t) * 2 + side], adj_sem.at[s, t, side])

    def load_step(i, carry):
        s = STEPS - 1 - i
        for side in (1, 0):
            for t in range(TREES):
                load(s, t, side).start()
        return carry

    lax.fori_loop(0, STEPS, load_step, 0)
    barrier_all(n)

    def to_partner(s, t):
        return remote(stage.at[s, t], total.at[s, t], dsend.at[s, t], drecv.at[s, t], partner)

    def to_parent(s, t, k):
        return remote(total.at[s, t], child.at[s - 1, t], csend.at[s, t], crecv.at[s, t], neighbour(t, k, core, chip))

    def give(s):
        for t in range(TREES):
            load(s, t, 1).wait()
            stage[s, t] = jnp.dot(u_ref[...], adj_v[(s * TREES + t) * 2 + 1], preferred_element_type=jnp.float32)
            to_partner(s, t).start()

    def take(s):
        for t in range(TREES):
            load(s, t, 0).wait()
            mine = jnp.dot(u_ref[...], adj_v[(s * TREES + t) * 2], preferred_element_type=jnp.float32)
            to_partner(s, t).wait_recv()
            total[s, t] = total[s, t] + mine
            for k in range(3):
                @pl.when(s < 2 ** k)
                def _():
                    to_parent(s + 2 ** k, t, k).wait_recv()
                    total[s, t] = total[s, t] + child[s + 2 ** k - 1, t]
            for k in range(3):
                @pl.when((s >= 2 ** k) & (s < 2 ** (k + 1)))
                def _():
                    to_parent(s, t, k).start()

    def step(i, carry):
        @pl.when(i < STEPS)
        def _():
            give(STEPS - 1 - i)

        @pl.when(i > 0)
        def _():
            take(STEPS - i)
        return carry

    lax.fori_loop(0, STEPS + 1, step, 0)
    feats = s_ref.shape[0]
    start = -(-feats // 8) * 8
    grad = []
    for t in range(TREES):
        cols = slice(t * width, (t + 1) * width)
        grad.append(jnp.where(z_ref[:, cols] > 0.0, total[0, t], 0.0).astype(jnp.bfloat16))
    part[0:feats] = lax.dot_general(s_ref[...], jnp.concatenate(grad, axis=1), COL_CONTRACT, preferred_element_type=jnp.float32)
    extra = small_ref.shape[0]
    part[feats:start] = jnp.zeros((start - feats, part.shape[1]), jnp.float32)
    part[start:start + extra] = small_ref[...]
    part[start + extra:] = jnp.zeros_like(part[start + extra:])
    share = part.shape[0] // n

    def rows_of(to):
        return part.at[pl.ds(pl.multiple_of(to * share, 8), share)]

    send_all(n, rows_of, parts.at[me], fsend, frecv)
    parts[me] = part[pl.ds(pl.multiple_of(me * share, 8), share)]

    def drain(s, carry):
        for t in range(TREES):
            to_partner(s, t).wait_send()

            @pl.when(s > 0)
            def _():
                to_parent(s, t, 0).wait_send()
        return carry

    lax.fori_loop(0, STEPS, drain, 0)
    wait_all(n, rows_of, parts.at[me], fsend, frecv)
    mine = whole.at[pl.ds(pl.multiple_of(me * share, 8), share)]
    mine[...] = jnp.sum(parts[...], axis=0)
    send_all(n, lambda to: mine, mine, gsend, grecv)
    wait_all(n, lambda to: mine, mine, gsend, grecv)
    dw_ref[...] = whole[0:feats]
    dw2_ref[...] = whole[start:start + dw2_ref.shape[0]]
    loss_ref[...] = whole[start + extra - 8:start + extra]


def backward(classes, u, s, z, small, adj):
    rows, nodes = adj.shape
    n = nodes // rows
    hidden, feats = u.shape[0], s.shape[0]
    width = rows // TREES
    share = -(-(-(-feats // 8) * 8 + small.shape[0]) // (8 * n)) * 8
    vmem = pl.BlockSpec(memory_space=pltpu.VMEM)
    dma = pltpu.SemaphoreType.DMA
    block = (TREES, hidden, width)
    return pl.pallas_call(
        functools.partial(backward_kernel, n),
        name='backward',
        out_shape=(jax.ShapeDtypeStruct((8, hidden), jnp.float32), jax.ShapeDtypeStruct((feats, hidden), jnp.float32), jax.ShapeDtypeStruct((classes, hidden), jnp.float32)),
        in_specs=[vmem] * 4 + [pl.BlockSpec(memory_space=pl.ANY)],
        out_specs=(vmem,) * 3,
        scratch_shapes=[
            pltpu.VMEM((2 * n // 2 * TREES, rows, width), jnp.bfloat16), pltpu.VMEM((STEPS, *block), jnp.float32), pltpu.VMEM((STEPS, *block), jnp.float32),
            pltpu.VMEM((STEPS - 1, *block), jnp.float32), pltpu.VMEM((n * share, hidden), jnp.float32), pltpu.VMEM((n, share, hidden), jnp.float32),
            pltpu.VMEM((n * share, hidden), jnp.float32), dma((STEPS, TREES, 2)), dma((STEPS, TREES)), dma((STEPS, TREES)), dma((STEPS, TREES)), dma((STEPS, TREES)),
            dma((n,)), dma((n,)), dma((n,)), dma((n,))],
        compiler_params=pltpu.CompilerParams(collective_id=1, has_side_effects=True, vmem_limit_bytes=67043328),
        cost_estimate=pl.CostEstimate(flops=2 * rows * nodes * hidden, bytes_accessed=2 * rows * nodes, transcendentals=0),
    )(u, s, z, small, adj)


def solution(mesh):
    axis_name = AXIS

    def local_step(adj_rows, feat_rows, w_one, w_two, label_rows, mask_rows):
        rows = adj_rows.shape[0]
        s, z, u, small = forward(feat_rows.T, w_one, w_two.T, label_rows.reshape(1, rows), mask_rows.reshape(1, rows), adj_rows)
        loss, dw_one, dw_two = backward(w_two.shape[1], u, s, z, small, adj_rows)
        return loss[0, 0:1], dw_one, dw_two.T

    return jax.shard_map(local_step, mesh=mesh, in_specs=(P(axis_name, None), P(axis_name, None), P(None, None), P(None, None), P(axis_name), P(axis_name)), out_specs=(P(None), P(None, None), P(None, None)), check_vma=False)
```

time: 368 us -> 174 us (0.47)
  waiting for transfers between devices: 162 us -> 0 us
  Pallas kernels: 79.7 us -> 168 us
  blocking collectives: 63.6 us -> 0 us
  matrix products: 35.9 us -> 0 us
  between operations: 17 us -> 0.65 us
    reduce_scatter x1 -> x0, waiting for transfers between devices: 93.7 us -> none  [local_step(): lax.psum_scatter(part_sums, axis_name, scatter_dimension=0, tiled=True)]
    pallas_call x1 -> x2, Pallas kernels: 79.7 us -> 168 us  [the longest x1 115 us: forward(): pl.pallas_call(functools.partial(forward_kernel, n), name='forward', out_...]
    psum x2 -> x0, blocking collectives: 63.6 us -> none  [the longest x1 31.9 us: local_step(): label_count = lax.psum(jnp.sum(weight), axis_name)]
    dot_general x5 -> x0, matrix products: 35.9 us -> none  [the longest x1 16.7 us: local_step(): lax.dot_general(adj_rows, back_two, ROW_CONTRACT, preferred_element_type=...]
    all_gather x1 -> x0, waiting for transfers between devices: 35.8 us -> none  [local_step(): hidden_all = lax.all_gather(hidden, axis_name, tiled=True, axis=1)]
    psum x1 -> x0, waiting for transfers between devices: 32.3 us -> none  [local_step(): lax.psum(lax.dot_general(agg_one, grad_one, (((1,), (0,)), ((), ())), pre...]
  transfers between devices with their start and end apart: 3 -> 0, of which waited for: 3 -> 0; matrix products, arithmetic and copies ran while one was open for 0% -> 0% of each run, Pallas kernels for 0% -> 0%
where the time goes in v2:
time: 174 us; the launch traced here: 173 us
  Pallas kernels  168 us (97%)
  local copies, waits for them, and re-layouts  4.25 us (2%)
    pallas_call x1, Pallas kernels, forward(): pl.pallas_call(functools.partial(forward_kernel, n), name='forward', out_...  115 us
    pallas_call x1, Pallas kernels, backward(): pl.pallas_call(functools.partial(backward_kernel, n), name='backward', ou...  53.2 us

profile of v2, /device:TPU:0, one launch (start us, length us, event | category | flops | bytes accessed | tf_op | source)
XLA Modules:
  0.0 173.3 jit_solution(3712096935688142221)
XLA Ops:
  0.6 115.2 %forward.1 = (bf16[602,1024]{1,0:T(8,128)(2,1)}, f32[128,1024]{1,0:T(8,128)}, bf16[128,1024]{1,0:T(8,128)(2,1)}, f32[56,128]{1,0:T(8,128)}) custom-call(bf16[602,1024]{1,0:T(8,128)(2,1)} %bitcast.7, f32[602,128]{1,0:T(8,128)} %w_ref.1, f32[41,128]{1,0:T(8,128)} %bitcast.8, s32[1,1024]{1,0:T(1,128)} %bitcast.9, s32[1,1024]{1,0:T(1,128)} %bitcast.10, ...), custom_call_target="tpu_custom_call" | custom-call | flops 24494735360 | bytes 33554432 | tf_op jit(solution)/shard_map/forward/pallas_call | solution.py:212
  115.8 53.2 %backward.1 = (f32[8,128]{1,0:T(8,128)}, f32[602,128]{1,0:T(8,128)}, f32[41,128]{1,0:T(8,128)}) custom-call(bf16[128,1024]{1,0:T(8,128)(2,1)} %get-tuple-element.10.u_ref, bf16[602,1024]{1,0:T(8,128)(2,1)} %get-tuple-element.11.s_ref, f32[128,1024]{1,0:T(8,128)} %get-tuple-element.12.z_ref, f32[56,128]{1,0:T(8,128)} %get-tuple-element.13.small_ref, ...), custom_call_target="tpu_custom_call" | custom-call | flops 4294967296 | bytes 33554432 | tf_op jit(solution)/shard_map/backward/pallas_call | solution.py:336
  169.1 1.2 slice.3
  170.3 1.7 copy.11
  172.0 1.3 copy.12
